TPU v7x, 32 devices: a 4x2x2 block of a 4x4x8 slice. The times are simulated.
32 devices in a mesh: dp: 4 (over y, z), vp: 8 (over x, core).
Axes of the slice: x: 4, y: 2, z: 2, core: 2. Of those that a mesh axis runs over, the one named last changes fastest.
The devices are a block of a 4x4x8 slice.
Arguments:
- hidden: bfloat16 [8192, 3584], P(('dp', 'vp')), parts along dimension 0
- target: int32 [8192], P('dp'), parts along dimension 0
- norm_gain: bfloat16 [3584], replicated
- head_weight: bfloat16 [3584, 152064], P(None, 'vp')
Outputs:
- output 1: float32 [8192], P('dp'), parts along dimension 0
- output 2: float32 [8192], P('dp'), parts along dimension 0
- output 3: float32 [4], P('dp'), parts along dimension 0
There are 4 independent parts. A program takes and returns all parts, laid end to end along the dimension named above; an argument that names none is the same for every part.
All inputs are finite; a program needn't handle non-finite values.
Results may differ from a plain program's by a relative error of at most 0.001.
Values are sent between devices in bfloat16 or wider.
A program may use at most 768 MiB of HBM per device.

v0:
```python
import jax
import jax.numpy as jnp
from jax import lax
from jax.sharding import PartitionSpec as P

NORM_EPS = 1e-6


def solution(mesh):
    def local_step(hidden, target, norm_gain, head_weight):
        hidden_f32 = hidden.astype(jnp.float32)
        inv_rms = lax.rsqrt(jnp.mean(hidden_f32 * hidden_f32, axis=-1, keepdims=True) + NORM_EPS)
        normed = (hidden_f32 * inv_rms * norm_gain.astype(jnp.float32)).astype(jnp.bfloat16)
        group_rows = lax.all_gather(normed, "vp", axis=0, tiled=True)
        logits = jnp.dot(group_rows, head_weight, preferred_element_type=jnp.float32)
        vocab_local = head_weight.shape[1]
        local_ids = target - lax.axis_index("vp") * vocab_local
        row_max = lax.pmax(jnp.max(logits, axis=-1), "vp")
        shifted = logits - row_max[:, None]
        exp_vals = jnp.exp(shifted)
        col_ids = jnp.arange(vocab_local, dtype=jnp.int32)
        target_shift = jnp.sum(jnp.where(col_ids[None, :] == local_ids[:, None], shifted, 0.0), axis=-1)
        local_stats = jnp.stack([jnp.sum(exp_vals, axis=-1), jnp.sum(exp_vals * shifted, axis=-1), target_shift])
        row_stats = lax.psum(local_stats, "vp")
        log_total = jnp.log(row_stats[0])
        log_prob = row_stats[2] - log_total
        entropy = log_total - row_stats[1] / row_stats[0]
        return log_prob, entropy, jnp.mean(log_prob).reshape(1)

    return jax.shard_map(local_step, mesh=mesh, in_specs=(P(("dp", "vp"), None), P("dp"), P(None), P(None, "vp")), out_specs=(P("dp"), P("dp"), P("dp")), check_vma=False)
```

profile of v0, /device:TPU:88, one launch (start us, length us, event | category | flops | bytes accessed | tf_op | source)
XLA Modules:
  0.0 491.7 jit_solution(5305455043410118879)
XLA Ops:
  7.2 0.1 all-gather.2.cloned.1.call-start
  7.2 0.7 convert_element_type.10
  7.9 1.9 fusion.1
  9.9 3.3 fusion.3
  13.2 0.1 all-gather.2.cloned.1.call-update
  13.2 1.3 broadcast_subtract_fusion
  14.5 74.8 %all-gather.2.cloned.1.call-done = bf16[2048,3584]{1,0:T(8,128)(2,1)} async-done(((bf16[256,3584]{1,0:T(8,128)(2,1)}), bf16[2048,3584]{1,0:T(8,128)(2,1)}) %all-gather.2.cloned.1.call-update) | async-done | bytes 14680080 | tf_op jit(solution)/shard_map/all_gather | solution.py:14
  89.3 0.0 copy-start
  89.3 297.5 %fusion.6 = (f32[2048]{0:T(1024)S(1)}, f32[2048,19008]{0,1:T(8,128)}) fusion(bf16[2048,3584]{1,0:T(8,128)(2,1)} %all-gather.2.cloned.1.call-done, bf16[3584,19008]{0,1:T(8,128)(2,1)} %param.7), kind=kOutput, calls=%fused_computation.18 | convolution fusion | flops 279077584896 | bytes 306651136 | tf_op jit(solution)/shard_map/dot_general | solution.py:15
  386.8 13.8 %pmax.7 = f32[2048]{0:T(1024)S(1)} all-reduce(f32[2048]{0:T(1024)S(1)} %get-tuple-element.9), channel_id=1, replica_groups=mesh['dp'=4,'vp'=8] {'vp'}, use_global_device_ids=true, to_apply=%region_2.0 | all-reduce | flops 2048 | bytes 16384 | tf_op jit(solution)/shard_map/pmax | solution.py:18
  400.7 0.0 copy-done
  400.7 57.4 %exponential_reduce_fusion = (f32[2048]{0:T(1024)S(1)}, f32[2048]{0:T(1024)S(1)}, f32[2048]{0:T(1024)S(1)}) fusion(f32[2048,19008]{0,1:T(8,128)} %get-tuple-element.10, f32[2048]{0:T(1024)S(1)} %pmax.7, s32[2048]{0:T(1024)S(1)} %copy-done), kind=kLoop, calls=%fused_computation.1 | loop fusion | flops 272492544 | bytes 155754496 | tf_op jit(solution)/shard_map/reduce_sum | solution.py:23
  458.1 23.7 %psum.7 = f32[3,2048]{1,0:T(4,128)S(1)} all-reduce(f32[3,2048]{1,0:T(4,128)S(1)} %pad_maximum_fusion), channel_id=1, replica_groups=mesh['dp'=4,'vp'=8] {'vp'}, use_global_device_ids=true, to_apply=%region_6.7 | all-reduce | flops 6144 | bytes 49152 | tf_op jit(solution)/shard_map/psum | solution.py:24
  481.8 1.2 fusion.5
  (2 shorter events, 0.0 us)
Async XLA Ops:
  7.2 82.1 %all-gather.2.cloned.1.call-start = ((), (), s32[]{:S(2)}) async-start(), calls=%async_computation | async-start | bytes 16515072 | tf_op jit(solution)/shard_map/all_gather | solution.py:14
  89.3 311.4 %copy-start = (s32[2048]{0:T(1024)S(1)}, s32[2048]{0:T(1024)}, u32[]{:S(2)}) copy-start(s32[2048]{0:T(1024)} %broadcast_subtract_fusion) | copy-start | bytes 24580
Sparse Core Ops, SparseCore 0:
  13.4 75.8 all-gather.1
where the time goes:
time: 492 us
  matrix products  298 us (61%)
  waiting for transfers between devices  74.8 us (15%)
  other arithmetic  65.9 us (13%)
  blocking collectives  37.5 us (8%)
  between operations  15.9 us (3%)
    dot_general x1, matrix products, local_step(): jnp.dot(group_rows, head_weight, preferred_element_type=jnp.float32)  298 us
    all_gather x1, waiting for transfers between devices, local_step(): group_rows = lax.all_gather(normed, 'vp', axis=0, tiled=True)  74.8 us
    reduce_sum x1, other arithmetic, local_step(): jnp.sum(exp_vals, axis=-1)  57.4 us
    psum x1, blocking collectives, local_step(): row_stats = lax.psum(local_stats, 'vp')  23.7 us
    pmax x1, blocking collectives, local_step(): row_max = lax.pmax(jnp.max(logits, axis=-1), 'vp')  13.8 us
  transfers between devices with their start and end apart: 1, of which 1 were waited for; matrix products, arithmetic and copies ran while one was open for 0% of the time, Pallas kernels for 0%

commit v1 on v0

v1 whole, which is shorter than its diff:
```python
import functools

import jax
import jax.numpy as jnp
from jax import lax
from jax.experimental import pallas as pl
from jax.experimental.pallas import tpu as pltpu
from jax.sharding import PartitionSpec as P

NORM_EPS = 1e-6
LANES = 128
SUBLANES = 8
SUB = 528
PER_TILE = 2
NBUF = 4
LOWEST = float(jnp.finfo(jnp.float32).min)
MESH = pl.DeviceIdType.MESH


def kernel(
    n_dev, hidden_ref, target_ref, gain_ref, head_ref,
    lp_ref, ent_ref, mean_ref,
    rows_ref, w_ref, m_ref, z_ref, s_ref, t_ref, id_ref, buf_a, buf_b, pack_ref, all_ref,
    w_sem, send_sem, recv_sem, st_send, st_recv,
):
    own = hidden_ref.shape[0]
    half = own // 2
    chip_rows = 2 * own
    n_chip = n_dev // 2
    vocab = head_ref.shape[0]
    tile = PER_TILE * SUB
    tiles = vocab // tile
    pairs = tiles // 2
    groups = chip_rows // LANES
    me = lax.axis_index("vp")
    core = lax.rem(me, 2)
    chip = me // 2
    partner = me + 1 - 2 * core
    right = lax.rem(me + 2, n_dev)
    left = lax.rem(me + n_dev - 2, n_dev)

    def w_copy(g):
        row = lax.rem(g, tiles) * tile
        slot = lax.rem(g, NBUF)
        return pltpu.make_async_copy(
            head_ref.at[pl.ds(pl.multiple_of(row, tile), tile), :], w_ref.at[slot], w_sem.at[slot]
        )

    w_copy(0).start()
    w_copy(1).start()

    barrier = pltpu.get_barrier_semaphore()
    for j in range(1, n_dev):
        pl.semaphore_signal(barrier, inc=1, device_id={"vp": lax.rem(me + j, n_dev)}, device_id_type=MESH)

    gain = gain_ref[...].astype(jnp.float32).reshape(1, gain_ref.shape[-1])
    step = 32

    def norm(i, carry):
        x = hidden_ref[pl.ds(pl.multiple_of(i * step, step), step), :].astype(jnp.float32)
        inv = lax.rsqrt(jnp.mean(x * x, axis=-1, keepdims=True) + NORM_EPS)
        rows_ref[0, pl.ds(pl.multiple_of(core * own + i * step, step), step), :] = (x * inv * gain).astype(jnp.bfloat16)
        return carry

    lax.fori_loop(0, own // step, norm, 0)
    pl.semaphore_wait(barrier, n_dev - 1)

    def remote(src, dst, idx, device):
        return pltpu.make_async_remote_copy(
            src_ref=src, dst_ref=dst, send_sem=send_sem.at[idx], recv_sem=recv_sem.at[idx],
            device_id={"vp": device}, device_id_type=MESH,
        )

    mine = pl.multiple_of(core * own, own)

    def piece(slot, part):
        return rows_ref.at[slot, pl.ds(pl.multiple_of(core * own + part * half, half), half), :]

    whole = rows_ref.at[0, pl.ds(mine, own), :]
    to_partner = remote(whole, whole, 0, partner)
    right_a = remote(piece(0, 0), piece(3, 0), 1, right)
    left_b = remote(piece(0, 1), piece(1, 1), 2, left)
    right_b = remote(piece(0, 1), piece(3, 1), 3, right)
    left_a = remote(piece(0, 0), piece(1, 0), 4, left)
    fwd_a = remote(piece(3, 0), piece(2, 0), 5, right)
    fwd_b = remote(piece(1, 1), piece(2, 1), 6, left)
    relay = [
        remote(piece(slot, part), piece(slot, part), 7 + i, partner)
        for i, (slot, part) in enumerate([(3, 0), (1, 1), (3, 1), (1, 0), (2, 0), (2, 1)])
    ]
    to_partner.start()
    right_a.start()
    left_b.start()
    right_b.start()
    left_a.start()

    sublane = lax.broadcasted_iota(jnp.int32, (SUBLANES, LANES), 0)
    for k in range(n_chip):
        src = lax.rem(chip + k, n_chip)
        for g in range(groups):
            ids = target_ref[src, pl.ds(g, 1), :] - me * vocab
            ids = jnp.where((ids >= 0) & (ids < vocab), ids, -(2**29))
            id_ref[k, :, pl.ds(g * LANES, LANES)] = ids - sublane
    m_ref[...] = jnp.full(m_ref.shape, LOWEST, jnp.float32)
    z_ref[...] = jnp.zeros(z_ref.shape, jnp.float32)
    s_ref[...] = jnp.zeros(s_ref.shape, jnp.float32)
    t_ref[...] = jnp.zeros(t_ref.shape, jnp.float32)
    buf_b[...] = jnp.full(buf_b.shape, LOWEST, jnp.float32)

    def epilogue(buf, k, base):
        n = SUB // SUBLANES
        for g in range(groups):
            ls = pl.ds(g * LANES, LANES)

            def logits(r):
                return buf[pl.ds(r * SUBLANES, SUBLANES), ls]

            tops = [functools.reduce(jnp.maximum, [logits(r) for r in range(q, n, 4)]) for q in range(4)]
            m_old = m_ref[k, :, ls]
            m_new = functools.reduce(jnp.maximum, tops, m_old)
            d = jnp.maximum(m_old - m_new, -200.0)
            a = jnp.exp(d)
            zv = z_ref[k, :, ls]
            sv = a * (s_ref[k, :, ls] + d * zv)
            zv = a * zv
            tv = t_ref[k, :, ls]
            ids = id_ref[k, :, ls] - base
            for r in range(n):
                v = logits(r)
                d = v - m_new
                p = jnp.exp(d)
                zv = zv + p
                sv = sv + p * d
                tv = jnp.where(ids == r * SUBLANES, v, tv)
            m_ref[k, :, ls] = m_new
            z_ref[k, :, ls] = zv
            s_ref[k, :, ls] = sv
            t_ref[k, :, ls] = tv

    def block(k, slot, c, buf):
        buf[...] = lax.dot_general(
            w_ref[slot, pl.ds(c, SUB), :], rows_ref[k], (((1,), (1,)), ((), ())), preferred_element_type=jnp.float32
        )

    bufs = (buf_a, buf_b)

    to_partner.wait_recv()

    def first(i, carry):
        w_copy(2 * i + 2).start()
        w_copy(2 * i + 3).start()

        @pl.when(i == pairs * 3 // 9)
        def _():
            right_a.wait_recv()
            left_b.wait_recv()
            fwd_a.start()
            fwd_b.start()
            relay[0].start()
            relay[1].start()

        @pl.when(i == pairs * 6 // 9)
        def _():
            right_b.wait_recv()
            left_a.wait_recv()
            relay[2].start()
            relay[3].start()

        @pl.when(i == pairs - 1)
        def _():
            fwd_a.wait_recv()
            fwd_b.wait_recv()
            relay[4].start()
            relay[5].start()

        w_copy(2 * i).wait()
        w_copy(2 * i + 1).wait()
        for b in range(2 * PER_TILE):
            block(0, lax.rem(2 * i + b // PER_TILE, NBUF), (b % PER_TILE) * SUB, bufs[b % 2])
            epilogue(bufs[(b + 1) % 2], 0, i * 2 * tile + (b - 1) * SUB)
        return carry

    lax.fori_loop(0, pairs, first, 0)
    epilogue(buf_b, 0, vocab - SUB)
    buf_b[...] = jnp.full(buf_b.shape, LOWEST, jnp.float32)
    for r in relay:
        r.wait_recv()

    order = [(k, c) for c in range(0, tile, SUB) for k in range(1, n_chip)]

    def second(j, carry):
        g = tiles + j

        @pl.when(j < tiles - 2)
        def _():
            w_copy(g + 2).start()

        w_copy(g).wait()
        for b, (k, c) in enumerate(order):
            block(k, lax.rem(g, NBUF), c, bufs[b % 2])
            pk, pc = order[b - 1]
            epilogue(bufs[(b + 1) % 2], pk, j * tile + pc - (tile if b == 0 else 0))
        return carry

    lax.fori_loop(0, tiles, second, 0)
    epilogue(buf_b, n_chip - 1, vocab - SUB)

    for k in range(n_chip):
        dst = lax.rem(chip + k, n_chip)
        for g in range(groups):
            ls = pl.ds(g * LANES, LANES)
            m = m_ref[k, :, ls]
            top = jnp.max(m, axis=0, keepdims=True)
            d = jnp.maximum(m - top, -200.0)
            a = jnp.exp(d)
            zv = z_ref[k, :, ls]
            sv = s_ref[k, :, ls]
            pack_ref[dst, pl.ds(g, 1), :] = top
            pack_ref[dst, pl.ds(groups + g, 1), :] = jnp.sum(a * zv, axis=0, keepdims=True)
            pack_ref[dst, pl.ds(2 * groups + g, 1), :] = jnp.sum(a * (sv + d * zv), axis=0, keepdims=True)
            pack_ref[dst, pl.ds(3 * groups + g, 1), :] = jnp.sum(t_ref[k, :, ls], axis=0, keepdims=True)

    sends = []
    for j in range(1, n_dev):
        peer = lax.rem(me + j, n_dev)
        c = pltpu.make_async_remote_copy(
            src_ref=pack_ref, dst_ref=all_ref.at[j - 1], send_sem=st_send.at[j - 1], recv_sem=st_recv.at[j - 1],
            device_id={"vp": peer}, device_id_type=MESH,
        )
        c.start()
        sends.append(c)
    for c in sends:
        c.wait_recv()
    for c in (to_partner, right_a, left_b, right_b, left_a, fwd_a, fwd_b, *relay, *sends):
        c.wait_send()

    total = jnp.zeros((1, 1), jnp.float32)
    for a in range(n_chip):
        parts = [pack_ref[a]] + [all_ref[j, a] for j in range(n_dev - 1)]
        ms = [p[0:groups] for p in parts]
        top = functools.reduce(jnp.maximum, ms)
        zsum = jnp.zeros_like(top)
        ssum = jnp.zeros_like(top)
        tsum = jnp.zeros_like(top)
        for p, m in zip(parts, ms):
            d = jnp.maximum(m - top, -200.0)
            e = jnp.exp(d)
            zsum = zsum + e * p[groups : 2 * groups]
            ssum = ssum + e * (p[2 * groups : 3 * groups] + d * p[groups : 2 * groups])
            tsum = tsum + p[3 * groups : 4 * groups]
        logz = jnp.log(zsum)
        lp = (tsum - top) - logz
        lp_ref[a] = lp
        ent_ref[a] = logz - ssum / zsum
        total = total + jnp.sum(lp, keepdims=True)
    mean_ref[...] = total / (n_chip * chip_rows)


def solution(mesh):
    n_dev = mesh.shape["vp"]

    def local_step(hidden, target, norm_gain, head_weight):
        own, depth = hidden.shape
        n_chip = n_dev // 2
        chip_rows = 2 * own
        groups = chip_rows // LANES
        vmem = pl.BlockSpec(memory_space=pltpu.VMEM)
        f32 = jnp.float32
        stat = pltpu.VMEM((n_chip, SUBLANES, chip_rows), f32)
        lp, ent, mean = pl.pallas_call(
            functools.partial(kernel, n_dev),
            out_shape=[
                jax.ShapeDtypeStruct((n_chip, groups, LANES), f32),
                jax.ShapeDtypeStruct((n_chip, groups, LANES), f32),
                jax.ShapeDtypeStruct((1, 1), f32),
            ],
            in_specs=[vmem, vmem, vmem, pl.BlockSpec(memory_space=pl.ANY)],
            out_specs=[vmem, vmem, vmem],
            scratch_shapes=[
                pltpu.VMEM((n_chip, chip_rows, depth), jnp.bfloat16),
                pltpu.VMEM((NBUF, PER_TILE * SUB, depth), jnp.bfloat16),
                stat, stat, stat, stat,
                pltpu.VMEM((n_chip, SUBLANES, chip_rows), jnp.int32),
                pltpu.VMEM((SUB, chip_rows), f32),
                pltpu.VMEM((SUB, chip_rows), f32),
                pltpu.VMEM((n_chip, 4 * groups, LANES), f32),
                pltpu.VMEM((n_dev - 1, n_chip, 4 * groups, LANES), f32),
                pltpu.SemaphoreType.DMA((NBUF,)),
                pltpu.SemaphoreType.DMA((13,)),
                pltpu.SemaphoreType.DMA((13,)),
                pltpu.SemaphoreType.DMA((n_dev - 1,)),
                pltpu.SemaphoreType.DMA((n_dev - 1,)),
            ],
            compiler_params=pltpu.CompilerParams(
                collective_id=0, has_side_effects=True, vmem_limit_bytes=67043328
            ),
        )(hidden, target.reshape(n_chip, groups, LANES), norm_gain, head_weight.T)
        return lp.reshape(-1), ent.reshape(-1), mean.reshape(-1)

    return jax.shard_map(
        local_step,
        mesh=mesh,
        in_specs=(P(("dp", "vp"), None), P("dp"), P(None), P(None, "vp")),
        out_specs=(P("dp"), P("dp"), P("dp")),
        check_vma=False,
    )
```

time: 492 us -> 311 us (0.63)
  Pallas kernels: 0 us -> 305 us
  matrix products: 298 us -> 0 us
  waiting for transfers between devices: 74.8 us -> 0 us
  other arithmetic: 65.9 us -> 0 us
  blocking collectives: 37.5 us -> 0 us
  between operations: 15.9 us -> 2.4 us
    pallas_call x0 -> x1, Pallas kernels: none -> 305 us  [local_step(): pl.pallas_call(functools.partial(kernel, n_dev), out_shape=[jax.ShapeDtyp...]
    dot_general x1 -> x0, matrix products: 298 us -> none  [local_step(): jnp.dot(group_rows, head_weight, preferred_element_type=jnp.float32)]
    all_gather x1 -> x0, waiting for transfers between devices: 74.8 us -> none  [local_step(): group_rows = lax.all_gather(normed, 'vp', axis=0, tiled=True)]
    reduce_sum x3 -> x0, other arithmetic: 60.6 us -> none  [the longest x1 57.4 us: local_step(): jnp.sum(exp_vals, axis=-1)]
    psum x1 -> x0, blocking collectives: 23.7 us -> none  [local_step(): row_stats = lax.psum(local_stats, 'vp')]
    pmax x1 -> x0, blocking collectives: 13.8 us -> none  [local_step(): row_max = lax.pmax(jnp.max(logits, axis=-1), 'vp')]
  transfers between devices with their start and end apart: 1 -> 0, of which waited for: 1 -> 0; matrix products, arithmetic and copies ran while one was open for 0% -> 0% of each run, Pallas kernels for 0% -> 0%
where the time goes in v1:
time: 311 us; the launch traced here: 310 us
  Pallas kernels  305 us (98%)
    pallas_call x1, Pallas kernels, local_step(): pl.pallas_call(functools.partial(kernel, n_dev), out_shape=[jax.ShapeDtyp...  305 us

profile of v1, /device:TPU:88, one launch (start us, length us, event | category | flops | bytes accessed | tf_op | source)
XLA Modules:
  0.0 310.2 jit_solution(8704058762772501751)
XLA Ops:
  0.6 305.2 %shard_map.67 = (f32[4,4,128]{2,1,0:T(4,128)}, f32[4,4,128]{2,1,0:T(4,128)}, f32[1,1]{1,0:T(1,128)}) custom-call(bf16[256,3584]{1,0:T(8,128)(2,1)} %hidden_ref.1, s32[4,4,128]{2,1,0:T(4,128)} %bitcast.5, bf16[3584]{0:T(1024)(128)(2,1)} %gain_ref.1, bf16[19008,3584]{1,0:T(8,128)(2,1)} %bitcast.1.head_ref), custom_call_target="tpu_custom_call" | custom-call | tf_op jit(solution)/shard_map/pallas_call | solution.py:270
  305.8 1.3 copy.10
  307.1 1.3 copy.11
